TPU v7x, 32 devices: a whole 2x2x4 slice. The times are simulated.
32 devices in a mesh: dp: 4 (over x, core), fsdp: 8 (over z, y).
Axes of the slice: x: 2, y: 2, z: 4, core: 2. Of those that a mesh axis runs over, the one named last changes fastest.
Arguments:
- tokens: bfloat16 [25088, 1024], P(('dp', 'fsdp')), may hold values from -6 to 6
- scale_codes: int32 [128], P(('dp', 'fsdp')), may hold values from 0 to 15
- w_qkv: float32 [1024, 3072], P('fsdp'), may hold values from -0.1875 to 0.1875
- b_q: float32 [1024], P('fsdp'), may hold values from -3 to 3
- b_v: float32 [1024], P('fsdp'), may hold values from -3 to 3
- w_out: float32 [1024, 1024], P('fsdp'), may hold values from -1.5 to 1.5
- b_out: float32 [1024], P('fsdp'), may hold values from -3 to 3
- gain_one: float32 [1024], P('fsdp'), may hold values from 0.5 to 1.5
- shift_one: float32 [1024], P('fsdp'), may hold values from -2 to 2
- w_fc1: float32 [1024, 4096], P('fsdp'), may hold values from -0.1875 to 0.1875
- b_fc1: float32 [4096], P('fsdp'), may hold values from -3 to 3
- w_fc2: float32 [4096, 1024], P('fsdp'), may hold values from -0.09375 to 0.09375
- b_fc2: float32 [1024], P('fsdp'), may hold values from -3 to 3
- gain_two: float32 [1024], P('fsdp'), may hold values from 0.5 to 1.5
- shift_two: float32 [1024], P('fsdp'), may hold values from -2 to 2
- cotangent: bfloat16 [25088, 1024], P(('dp', 'fsdp')), may hold values from -6 to 6
Outputs:
- block_out: bfloat16 [25088, 1024], P(('dp', 'fsdp'))
- grad_tokens: float32 [25088, 1024], P(('dp', 'fsdp'))
- grad_w_qkv: float32 [1024, 3072], P('fsdp')
- grad_b_q: float32 [1024], P('fsdp')
- grad_b_v: float32 [1024], P('fsdp')
- grad_w_out: float32 [1024, 1024], P('fsdp')
- grad_b_out: float32 [1024], P('fsdp')
- grad_gain_one: float32 [1024], P('fsdp')
- grad_shift_one: float32 [1024], P('fsdp')
- grad_w_fc1: float32 [1024, 4096], P('fsdp')
- grad_b_fc1: float32 [4096], P('fsdp')
- grad_w_fc2: float32 [4096, 1024], P('fsdp')
- grad_b_fc2: float32 [1024], P('fsdp')
- grad_gain_two: float32 [1024], P('fsdp')
- grad_shift_two: float32 [1024], P('fsdp')
All inputs are finite; a program needn't handle non-finite values.
Results may differ from a plain program's by a relative error of at most 0.015.
Values may be sent and summed in bfloat16 or wider, within the bound.
No kernel may reach another device: no remote copies, remote signals or barrier semaphores. Data moves between devices by JAX's collectives and lax.ppermute only.
A program may use at most 256 MiB of HBM per device.

v0:
```python
import math
import jax
import jax.numpy as jnp
from jax import lax
from jax.sharding import PartitionSpec as P

HEADS = 16
GRID = 14
NSCALE = 16
norm_eps = 1e-06


def positions(codes, grid_side, width):
    ratio = 0.3 * jnp.exp(codes.astype(jnp.float32) * (math.log(10.0 / 0.3) / (NSCALE - 1)))
    quarter = width // 4
    omega = jnp.exp(jnp.arange(quarter).astype(jnp.float32) * (-math.log(10000.0) / quarter))
    cells = jnp.arange(grid_side * grid_side, dtype=jnp.int32)
    row_place = (cells // grid_side).astype(jnp.float32)
    col_place = (cells % grid_side).astype(jnp.float32)
    row_angle = ratio[:, None, None] * row_place[None, :, None] * omega[None, None, :]
    col_angle = ratio[:, None, None] * col_place[None, :, None] * omega[None, None, :]
    return jnp.concatenate(
        [jnp.sin(row_angle), jnp.cos(row_angle), jnp.sin(col_angle), jnp.cos(col_angle)], axis=-1
    )


def norm_affine(hidden, gain, shift):
    center = jnp.mean(hidden, axis=-1, keepdims=True)
    offset = hidden - center
    spread = jnp.mean(offset * offset, axis=-1, keepdims=True)
    return offset * lax.rsqrt(spread + norm_eps) * gain + shift


def matmul(left, right):
    return jnp.dot(left, right, preferred_element_type=jnp.float32)


def inner_rows(left, right):
    return lax.dot_general(
        left, right, (((0,), (0,)), ((), ())), preferred_element_type=jnp.float32
    )


def times_transposed(left, right):
    return lax.dot_general(
        left, right, (((1,), (1,)), ((), ())), preferred_element_type=jnp.float32
    )


def column_total(values):
    return jnp.sum(values.astype(jnp.float32), axis=0)


def local(
    tokens,
    scale_codes,
    w_qkv,
    b_q,
    b_v,
    w_out,
    b_out,
    gain_one,
    shift_one,
    w_fc1,
    b_fc1,
    w_fc2,
    b_fc2,
    gain_two,
    shift_two,
    cotangent,
):
    half = jnp.bfloat16
    row_count, width = tokens.shape
    n_img = scale_codes.shape[0]
    patches = row_count // n_img
    head_size = width // HEADS
    factor = 1.0 / math.sqrt(head_size)
    place = positions(scale_codes, GRID, width).reshape(row_count, width)
    x_zero = tokens.astype(jnp.float32) + place
    attn_params = (
        lax.all_gather(w_qkv.astype(half), "fsdp", axis=0, tiled=True),
        lax.all_gather(b_q.astype(half), "fsdp", axis=0, tiled=True),
        lax.all_gather(b_v.astype(half), "fsdp", axis=0, tiled=True),
        lax.all_gather(w_out.astype(half), "fsdp", axis=0, tiled=True),
        lax.all_gather(b_out.astype(half), "fsdp", axis=0, tiled=True),
        lax.all_gather(gain_one.astype(half), "fsdp", axis=0, tiled=True),
        lax.all_gather(shift_one.astype(half), "fsdp", axis=0, tiled=True),
    )
    full_qkv, full_bq, full_bv, full_out, full_bout, full_gone, full_sone = attn_params
    gain_one_f = full_gone.astype(jnp.float32)
    shift_one_f = full_sone.astype(jnp.float32)
    normed_one = norm_affine(x_zero, gain_one_f, shift_one_f).astype(half)
    qkv_bias = jnp.concatenate([full_bq, jnp.zeros_like(full_bq), full_bv]).astype(jnp.float32)
    projected = (
        (matmul(normed_one, full_qkv) + qkv_bias)
        .astype(half)
        .reshape(n_img, patches, 3, HEADS, head_size)
    )
    queries = projected[:, :, 0]
    keys_all = projected[:, :, 1]
    values_all = projected[:, :, 2]
    scores = (
        jnp.einsum("iqhd,ikhd->ihqk", queries, keys_all, preferred_element_type=jnp.float32)
        * factor
    )
    top_score = jnp.max(scores, axis=-1, keepdims=True)
    raised = jnp.exp(scores - top_score)
    totals = jnp.sum(raised, axis=-1, keepdims=True)
    probs = raised / totals
    log_total = top_score + jnp.log(totals)
    mixed = jnp.einsum(
        "ihqk,ikhd->iqhd", probs.astype(half), values_all, preferred_element_type=jnp.float32
    )
    mixed = mixed.reshape(row_count, width).astype(half)
    after_attn = x_zero + (matmul(mixed, full_out) + full_bout.astype(jnp.float32))
    mlp_params = (
        lax.all_gather(w_fc1.astype(half), "fsdp", axis=0, tiled=True),
        lax.all_gather(b_fc1.astype(half), "fsdp", axis=0, tiled=True),
        lax.all_gather(w_fc2.astype(half), "fsdp", axis=0, tiled=True),
        lax.all_gather(b_fc2.astype(half), "fsdp", axis=0, tiled=True),
        lax.all_gather(gain_two.astype(half), "fsdp", axis=0, tiled=True),
        lax.all_gather(shift_two.astype(half), "fsdp", axis=0, tiled=True),
    )
    full_fc1, full_bfc1, full_fc2, full_bfc2, full_gtwo, full_stwo = mlp_params
    gain_two_f = full_gtwo.astype(jnp.float32)
    shift_two_f = full_stwo.astype(jnp.float32)
    normed_two = norm_affine(after_attn, gain_two_f, shift_two_f).astype(half)
    hidden_pre = matmul(normed_two, full_fc1) + full_bfc1.astype(jnp.float32)
    hidden_act = jax.nn.gelu(hidden_pre, approximate=False).astype(half)
    block_out = (
        after_attn + (matmul(hidden_act, full_fc2) + full_bfc2.astype(jnp.float32))
    ).astype(half)
    back_mlp = (
        lax.all_gather(w_fc1.astype(half), "fsdp", axis=0, tiled=True),
        lax.all_gather(b_fc1.astype(half), "fsdp", axis=0, tiled=True),
        lax.all_gather(w_fc2.astype(half), "fsdp", axis=0, tiled=True),
        lax.all_gather(b_fc2.astype(half), "fsdp", axis=0, tiled=True),
        lax.all_gather(gain_two.astype(half), "fsdp", axis=0, tiled=True),
        lax.all_gather(shift_two.astype(half), "fsdp", axis=0, tiled=True),
    )
    back_fc1 = back_mlp[0]
    back_fc2 = back_mlp[2]
    back_gtwo = back_mlp[4].astype(jnp.float32)
    back_stwo = back_mlp[5].astype(jnp.float32)
    grad_w_fc2 = inner_rows(hidden_act, cotangent)
    grad_b_fc2 = column_total(cotangent)
    grad_act = times_transposed(cotangent, back_fc2)
    unused_act, gelu_pull = jax.vjp(lambda pre: jax.nn.gelu(pre, approximate=False), hidden_pre)
    grad_pre = gelu_pull(grad_act)[0].astype(half)
    grad_w_fc1 = inner_rows(normed_two, grad_pre)
    grad_b_fc1 = column_total(grad_pre)
    grad_two_in = times_transposed(grad_pre, back_fc1)
    unused_two, norm_two_pull = jax.vjp(norm_affine, after_attn, back_gtwo, back_stwo)
    part_two, grad_gain_two, grad_shift_two = norm_two_pull(grad_two_in)
    grad_after = cotangent.astype(jnp.float32) + part_two
    mlp_shards = (
        lax.psum_scatter(grad_w_fc1, "fsdp", scatter_dimension=0, tiled=True),
        lax.psum_scatter(grad_b_fc1, "fsdp", scatter_dimension=0, tiled=True),
        lax.psum_scatter(grad_w_fc2, "fsdp", scatter_dimension=0, tiled=True),
        lax.psum_scatter(grad_b_fc2, "fsdp", scatter_dimension=0, tiled=True),
        lax.psum_scatter(grad_gain_two, "fsdp", scatter_dimension=0, tiled=True),
        lax.psum_scatter(grad_shift_two, "fsdp", scatter_dimension=0, tiled=True),
    )
    back_attn = (
        lax.all_gather(w_qkv.astype(half), "fsdp", axis=0, tiled=True),
        lax.all_gather(b_q.astype(half), "fsdp", axis=0, tiled=True),
        lax.all_gather(b_v.astype(half), "fsdp", axis=0, tiled=True),
        lax.all_gather(w_out.astype(half), "fsdp", axis=0, tiled=True),
        lax.all_gather(b_out.astype(half), "fsdp", axis=0, tiled=True),
        lax.all_gather(gain_one.astype(half), "fsdp", axis=0, tiled=True),
        lax.all_gather(shift_one.astype(half), "fsdp", axis=0, tiled=True),
    )
    back_qkv = back_attn[0]
    back_out = back_attn[3]
    back_gone = back_attn[5].astype(jnp.float32)
    back_sone = back_attn[6].astype(jnp.float32)
    branch_grad = grad_after.astype(half)
    grad_w_out = inner_rows(mixed, branch_grad)
    grad_b_out = column_total(branch_grad)
    grad_mixed = (
        times_transposed(branch_grad, back_out)
        .astype(half)
        .reshape(n_img, patches, HEADS, head_size)
    )
    again_scores = (
        jnp.einsum("iqhd,ikhd->ihqk", queries, keys_all, preferred_element_type=jnp.float32)
        * factor
    )
    again_probs = jnp.exp(again_scores - log_total)
    grad_values = jnp.einsum(
        "ihqk,iqhd->ikhd", again_probs.astype(half), grad_mixed, preferred_element_type=jnp.float32
    )
    grad_probs = jnp.einsum(
        "iqhd,ikhd->ihqk", grad_mixed, values_all, preferred_element_type=jnp.float32
    )
    weighted = jnp.sum(again_probs * grad_probs, axis=-1, keepdims=True)
    grad_scores = (again_probs * (grad_probs - weighted)).astype(half)
    grad_queries = (
        jnp.einsum("ihqk,ikhd->iqhd", grad_scores, keys_all, preferred_element_type=jnp.float32)
        * factor
    )
    grad_keys = (
        jnp.einsum("ihqk,iqhd->ikhd", grad_scores, queries, preferred_element_type=jnp.float32)
        * factor
    )
    grad_proj = (
        jnp.stack([grad_queries, grad_keys, grad_values], axis=2)
        .reshape(row_count, 3 * width)
        .astype(half)
    )
    grad_w_qkv = inner_rows(normed_one, grad_proj)
    grad_b_q = column_total(grad_proj[:, :width])
    grad_b_v = column_total(grad_proj[:, 2 * width :])
    grad_one_in = times_transposed(grad_proj, back_qkv)
    unused_one, norm_one_pull = jax.vjp(norm_affine, x_zero, back_gone, back_sone)
    part_one, grad_gain_one, grad_shift_one = norm_one_pull(grad_one_in)
    grad_tokens = grad_after + part_one
    attn_shards = (
        lax.psum_scatter(grad_w_qkv, "fsdp", scatter_dimension=0, tiled=True),
        lax.psum_scatter(grad_b_q, "fsdp", scatter_dimension=0, tiled=True),
        lax.psum_scatter(grad_b_v, "fsdp", scatter_dimension=0, tiled=True),
        lax.psum_scatter(grad_w_out, "fsdp", scatter_dimension=0, tiled=True),
        lax.psum_scatter(grad_b_out, "fsdp", scatter_dimension=0, tiled=True),
        lax.psum_scatter(grad_gain_one, "fsdp", scatter_dimension=0, tiled=True),
        lax.psum_scatter(grad_shift_one, "fsdp", scatter_dimension=0, tiled=True),
    )
    summed = (
        lax.psum(attn_shards[0].astype(jnp.bfloat16), "dp").astype(jnp.float32),
        lax.psum(attn_shards[1].astype(jnp.bfloat16), "dp").astype(jnp.float32),
        lax.psum(attn_shards[2].astype(jnp.bfloat16), "dp").astype(jnp.float32),
        lax.psum(attn_shards[3].astype(jnp.bfloat16), "dp").astype(jnp.float32),
        lax.psum(attn_shards[4].astype(jnp.bfloat16), "dp").astype(jnp.float32),
        lax.psum(attn_shards[5].astype(jnp.bfloat16), "dp").astype(jnp.float32),
        lax.psum(attn_shards[6].astype(jnp.bfloat16), "dp").astype(jnp.float32),
        lax.psum(mlp_shards[0].astype(jnp.bfloat16), "dp").astype(jnp.float32),
        lax.psum(mlp_shards[1].astype(jnp.bfloat16), "dp").astype(jnp.float32),
        lax.psum(mlp_shards[2].astype(jnp.bfloat16), "dp").astype(jnp.float32),
        lax.psum(mlp_shards[3].astype(jnp.bfloat16), "dp").astype(jnp.float32),
        lax.psum(mlp_shards[4].astype(jnp.bfloat16), "dp").astype(jnp.float32),
        lax.psum(mlp_shards[5].astype(jnp.bfloat16), "dp").astype(jnp.float32),
    )
    return (
        block_out,
        grad_tokens,
        summed[0],
        summed[1],
        summed[2],
        summed[3],
        summed[4],
        summed[5],
        summed[6],
        summed[7],
        summed[8],
        summed[9],
        summed[10],
        summed[11],
        summed[12],
    )


def solution(mesh):
    placed = (
        P(("dp", "fsdp"), None),
        P(("dp", "fsdp")),
        P("fsdp", None),
        P("fsdp"),
        P("fsdp"),
        P("fsdp", None),
        P("fsdp"),
        P("fsdp"),
        P("fsdp"),
        P("fsdp", None),
        P("fsdp"),
        P("fsdp", None),
        P("fsdp"),
        P("fsdp"),
        P("fsdp"),
        P(("dp", "fsdp"), None),
    )
    return jax.shard_map(
        local,
        mesh=mesh,
        in_specs=placed,
        out_specs=(
            P(("dp", "fsdp"), None),
            P(("dp", "fsdp"), None),
            P("fsdp", None),
            P("fsdp"),
            P("fsdp"),
            P("fsdp", None),
            P("fsdp"),
            P("fsdp"),
            P("fsdp"),
            P("fsdp", None),
            P("fsdp"),
            P("fsdp", None),
            P("fsdp"),
            P("fsdp"),
            P("fsdp"),
        ),
        check_vma=False,
    )
```

profile of v0, /device:TPU:0, one launch (start us, length us, event | category | flops | bytes accessed | tf_op | source)
XLA Modules:
  0.0 1432.2 jit_solution(16230341930971764661)
XLA Ops:
  16.1 22.5 %all-gather.6 = bf16[8,1,128]{2,1,0:T(2,128)(2,1)S(1)} all-gather(bf16[1,1,128]{2,1,0:T(2,128)(2,1)S(1)} %convert_bitcast_fusion.3), channel_id=1, replica_groups=mesh['dp'=4,'fsdp'=8] {'fsdp'}, dimensions={0}, use_global_device_ids=true | all-gather | bytes 2304 | tf_op jit(solution)/shard_map/all_gather | solution.py:122
  38.6 16.3 %all-gather.5 = bf16[8,1,128]{2,1,0:T(2,128)(2,1)S(1)} all-gather(bf16[1,1,128]{2,1,0:T(2,128)(2,1)S(1)} %convert_bitcast_fusion.4), channel_id=1, replica_groups=mesh['dp'=4,'fsdp'=8] {'fsdp'}, dimensions={0}, use_global_device_ids=true | all-gather | bytes 2304 | tf_op jit(solution)/shard_map/all_gather | solution.py:121
  54.9 18.5 %all-gather.1 = bf16[8,1,128]{2,1,0:T(2,128)(2,1)S(1)} all-gather(bf16[1,1,128]{2,1,0:T(2,128)(2,1)S(1)} %convert_bitcast_fusion.8), channel_id=1, replica_groups=mesh['dp'=4,'fsdp'=8] {'fsdp'}, dimensions={0}, use_global_device_ids=true | all-gather | bytes 2304 | tf_op jit(solution)/shard_map/all_gather | solution.py:87
  73.4 16.4 %all-gather = bf16[8,1,128]{2,1,0:T(2,128)(2,1)S(1)} all-gather(bf16[1,1,128]{2,1,0:T(2,128)(2,1)S(1)} %convert_bitcast_fusion.9), channel_id=1, replica_groups=mesh['dp'=4,'fsdp'=8] {'fsdp'}, dimensions={0}, use_global_device_ids=true | all-gather | bytes 2304 | tf_op jit(solution)/shard_map/all_gather | solution.py:86
  89.9 18.4 %all-gather.4 = bf16[8,1,128]{2,1,0:T(2,128)(2,1)S(1)} all-gather(bf16[1,1,128]{2,1,0:T(2,128)(2,1)S(1)} %convert_bitcast_fusion.5), channel_id=1, replica_groups=mesh['dp'=4,'fsdp'=8] {'fsdp'}, dimensions={0}, use_global_device_ids=true | all-gather | bytes 2304 | tf_op jit(solution)/shard_map/all_gather | solution.py:85
  108.3 16.2 %all-gather.3 = bf16[8,1,128]{2,1,0:T(2,128)(2,1)S(1)} all-gather(bf16[1,1,128]{2,1,0:T(2,128)(2,1)S(1)} %convert_bitcast_fusion.6), channel_id=1, replica_groups=mesh['dp'=4,'fsdp'=8] {'fsdp'}, dimensions={0}, use_global_device_ids=true | all-gather | bytes 2304 | tf_op jit(solution)/shard_map/all_gather | solution.py:83
  124.5 18.2 %all-gather.2 = bf16[8,1,128]{2,1,0:T(2,128)(2,1)S(1)} all-gather(bf16[1,1,128]{2,1,0:T(2,128)(2,1)S(1)} %convert_bitcast_fusion.7), channel_id=1, replica_groups=mesh['dp'=4,'fsdp'=8] {'fsdp'}, dimensions={0}, use_global_device_ids=true | all-gather | bytes 2304 | tf_op jit(solution)/shard_map/all_gather | solution.py:82
  142.8 26.3 %all-gather.7 = bf16[8,1,512]{2,1,0:T(2,128)(2,1)S(1)} all-gather(bf16[1,1,512]{2,1,0:T(2,128)(2,1)S(1)} %reshape.247), channel_id=1, replica_groups=mesh['dp'=4,'fsdp'=8] {'fsdp'}, dimensions={0}, use_global_device_ids=true | all-gather | bytes 9216 | tf_op jit(solution)/shard_map/all_gather | solution.py:118
  187.9 12.7 reshape.267
  248.2 41.3 %all-gather.18.cloned.1.call-done = bf16[1024,4096]{1,0:T(8,128)(2,1)} async-done(((bf16[128,4096]{1,0:T(8,128)(2,1)}), bf16[1024,4096]{1,0:T(8,128)(2,1)}) %all-gather.18.cloned.1.call-update) | async-done | bytes 8388624 | tf_op jit(solution)/shard_map/all_gather | solution.py:117
  289.5 13.2 fusion.42
  302.7 112.5 %all-gather.20.cloned.1.call-done = bf16[4096,1024]{1,0:T(8,128)(2,1)} async-done(((bf16[512,1024]{1,0:T(8,128)(2,1)}), bf16[4096,1024]{1,0:T(8,128)(2,1)}) %all-gather.20.cloned.1.call-update) | async-done | bytes 8388624 | tf_op jit(solution)/shard_map/all_gather | solution.py:119
  415.2 41.3 %convert_reduce_fusion = (f32[4096]{0:T(1024)}, bf16[784,4096]{1,0:T(8,128)(2,1)}, f32[784,4096]{1,0:T(8,128)}) fusion(f32[784,4096]{1,0:T(8,128)} %fusion.42, f32[4096]{0:T(1024)S(1)} %bitcast.97, bf16[784,1024]{1,0:T(8,128)(2,1)S(1)} %copy-done.12, bf16[4096,1024]{1,0:T(8,128)(2,1)} %all-gather.20.cloned.1.call-done), kind=kOutput, calls=%fused_computation.7 | convolution fusion | flops 6817509376 | bytes 42139648 | tf_op jit(solution)/shard_map/dot_general | solution.py:45
  488.2 14.4 %multiply_reduce_fusion = (f32[4,16,196]{2,1,0:T(8,128)S(1)}, f32[4,16,196,196]{2,3,1,0:T(8,128)}) fusion(f32[4,16,196,196]{2,3,1,0:T(8,128)} %copy-done, f32[4,16,196]{2,1,0:T(8,128)S(1)} %log_add_fusion, bf16[4,196,16,64]{1,3,2,0:T(8,128)(2,1)} %copy.60, bf16[4,196,1,16,64]{1,4,3,0,2:T(8,128)(2,1)} %copy.74), kind=kOutput, calls=%fused_computation.2 | convolution fusion | flops 324525824 | bytes 22980608 | tf_op jit(solution)/shard_map/iqhd,ikhd->ihqk/dot_general | solution.py:193
  537.6 12.7 convert_element_type.285
  550.4 13.0 fusion.40
  564.1 15.8 %fusion.41 = f32[1024,4096]{1,0:T(8,128)} fusion(bf16[784,4096]{1,0:T(8,128)(2,1)} %get-tuple-element.46, f32[784,1024]{1,0:T(8,128)} %copy-done.7, f32[1024]{0:T(1024)S(1)} %bitcast.110, f32[1024]{0:T(1024)S(1)} %bitcast.106, f32[784]{0:T(1024)S(1)} %fusion.33, f32[784]{0:T(1024)S(1)} %broadcast_multiply_fusion), kind=kOutput, calls=%fused_computation.116 | convolution fusion | flops 6580682752 | bytes 26425472 | tf_op jit(solution)/shard_map/dot_general | solution.py:39
  606.7 18.6 %all-gather.8 = bf16[8,1,128]{2,1,0:T(2,128)(2,1)S(1)} all-gather(bf16[1,1,128]{2,1,0:T(2,128)(2,1)S(1)} %convert_bitcast_fusion.2), channel_id=1, replica_groups=mesh['dp'=4,'fsdp'=8] {'fsdp'}, dimensions={0}, use_global_device_ids=true | all-gather | bytes 2304 | tf_op jit(solution)/shard_map/all_gather | solution.py:120
  642.7 36.8 %all-reduce.9 = (bf16[1024]{0:T(1024)(128)(2,1)S(1)}, bf16[1024]{0:T(1024)(128)(2,1)S(1)}, bf16[1024]{0:T(1024)(128)(2,1)S(1)}, bf16[1024]{0:T(1024)(128)(2,1)S(...) all-reduce(f32[1024]{0:T(1024)S(1)} %get-tuple-element.20, ...), channel_id=3, replica_groups=mesh['dp'=4,'fsdp'=8] {'fsdp'}, use_global_device_ids=true, to_apply=%region_14.15.clone | all-reduce | flops 12288 | bytes 73728
  693.0 80.1 %reduce-scatter.5.cloned.1.call-done = f32[128,3072]{1,0:T(8,128)} async-done(((f32[1024,3072]{1,0:T(8,128)}), f32[128,3072]{1,0:T(8,128)}) %reduce-scatter.5.cloned.1.call-update) | async-done | bytes 1572880 | tf_op jit(solution)/shard_map/reduce_scatter | solution.py:219
  775.5 283.7 %reduce-scatter.9.cloned.1.call-done = f32[128,4096]{1,0:T(8,128)} async-done(((f32[1024,4096]{1,0:T(8,128)}), f32[128,4096]{1,0:T(8,128)}) %reduce-scatter.9.cloned.1.call-update) | async-done | bytes 2097168 | tf_op jit(solution)/shard_map/reduce_scatter | solution.py:157
  1061.9 282.9 %reduce-scatter.11.cloned.1.call-done = f32[512,1024]{1,0:T(8,128)} async-done(((f32[4096,1024]{1,0:T(8,128)}), f32[512,1024]{1,0:T(8,128)}) %reduce-scatter.11.cloned.1.call-update) | async-done | bytes 2097168 | tf_op jit(solution)/shard_map/reduce_scatter | solution.py:159
  1347.6 12.0 add_convert_fusion.2
  1359.5 57.2 %all-reduce.14.cloned.1.call-done = (bf16[128,3072]{1,0:T(8,128)(2,1)}, bf16[128,1024]{1,0:T(8,128)(2,1)}, bf16[128,4096]{1,0:T(8,128)(2,1)}, bf16[512,1024]{1,0:T(8,128)(2,1)}) async-done(((bf16[128,3072]{1,0:T(8,128)(2,1)}, bf16[128,1024]{1,0:T(8,128)(2,1)}, bf16[128,4096]{1,0:T(8,128)(2,1)}, bf16[512,1024]{1,0:T(8,128)(2,1)}), (bf16[128,3072]{1,0:T(8,128)(2,1)}, bf16[128,1024]{1,0:T(8,128)(2,1)}, ...) | async-done | bytes 3145744 | tf_op jit(solution)/shard_map/psum | solution.py:228
  (235 shorter events, 215.2 us)
Async XLA Ops:
  7.2 170.1 %all-gather.14.cloned.1.call-start = ((), (), s32[]{:S(2)}) async-start(), calls=%async_computation.4 | async-start | bytes 7077888 | tf_op jit(solution)/shard_map/all_gather | solution.py:81
  9.8 232.0 %all-gather.16.cloned.1.call-start = ((), (), s32[]{:S(2)}) async-start(), calls=%async_computation.5 | async-start | bytes 2359296 | tf_op jit(solution)/shard_map/all_gather | solution.py:84
  11.7 26.9 %copy-start.40 = (f32[128]{0:T(128)S(1)}, f32[128]{0:T(128)}, u32[]{:S(2)}) copy-start(f32[128]{0:T(128)} %param.29) | copy-start | bytes 1540
  11.7 43.2 %copy-start.41 = (f32[128]{0:T(128)S(1)}, f32[128]{0:T(128)}, u32[]{:S(2)}) copy-start(f32[128]{0:T(128)} %param.24) | copy-start | bytes 1540
  11.7 61.7 %copy-start.42 = (f32[128]{0:T(128)S(1)}, f32[128]{0:T(128)}, u32[]{:S(2)}) copy-start(f32[128]{0:T(128)} %param.23) | copy-start | bytes 1540
  11.7 78.1 %copy-start.43 = (f32[128]{0:T(128)S(1)}, f32[128]{0:T(128)}, u32[]{:S(2)}) copy-start(f32[128]{0:T(128)} %param.22) | copy-start | bytes 1540
  11.7 96.5 %copy-start.44 = (f32[128]{0:T(128)S(1)}, f32[128]{0:T(128)}, u32[]{:S(2)}) copy-start(f32[128]{0:T(128)} %param.20) | copy-start | bytes 1540
  11.7 112.7 %copy-start.45 = (f32[128]{0:T(128)S(1)}, f32[128]{0:T(128)}, u32[]{:S(2)}) copy-start(f32[128]{0:T(128)} %param.19) | copy-start | bytes 1540
  11.7 130.9 %copy-start.46 = (s32[4]{0:T(128)S(1)}, s32[4]{0:T(128)}, u32[]{:S(2)}) copy-start(s32[4]{0:T(128)} %param.17) | copy-start | bytes 52
  11.7 277.7 %all-gather.18.cloned.1.call-start = ((), (), s32[]{:S(2)}) async-start(), calls=%async_computation.6 | async-start | bytes 9437184 | tf_op jit(solution)/shard_map/all_gather | solution.py:117
  12.9 402.3 %all-gather.20.cloned.1.call-start = ((), (), s32[]{:S(2)}) async-start(), calls=%async_computation.7 | async-start | bytes 9437184 | tf_op jit(solution)/shard_map/all_gather | solution.py:119
  15.7 675.5 %reduce-scatter.7.cloned.1.call-start = ((), (), s32[]{:S(2)}) async-start(), calls=%async_computation.9 | async-start | bytes 4718592 | tf_op jit(solution)/shard_map/reduce_scatter | solution.py:222
  38.5 250.9 %copy-start.33 = (f32[8,1,128]{2,1,0:T(1,128)}, f32[8,1,128]{2,1,0:T(1,128)S(1)}, u32[]{:S(2)}) copy-start(f32[8,1,128]{2,1,0:T(1,128)S(1)} %convert_element_type.320) | copy-start | bytes 12292
  73.4 103.9 %copy-start.35 = (f32[8,1,128]{2,1,0:T(1,128)}, f32[8,1,128]{2,1,0:T(1,128)S(1)}, u32[]{:S(2)}) copy-start(f32[8,1,128]{2,1,0:T(1,128)S(1)} %convert_element_type.317) | copy-start | bytes 12292
  89.8 87.5 %copy-start.28 = (f32[8,1,128]{2,1,0:T(1,128)}, f32[8,1,128]{2,1,0:T(1,128)S(1)}, u32[]{:S(2)}) copy-start(f32[8,1,128]{2,1,0:T(1,128)S(1)} %convert_element_type.316) | copy-start | bytes 12292
  248.2 54.5 %copy-start.26 = (f32[784]{0:T(1024)}, f32[784]{0:T(1024)S(1)}, u32[]{:S(2)}) copy-start(f32[784]{0:T(1024)S(1)} %multiply_reduce_fusion.6) | copy-start | bytes 9412
  289.5 125.7 %copy-start.12 = (bf16[784,1024]{1,0:T(8,128)(2,1)S(1)}, bf16[784,1024]{1,0:T(8,128)(2,1)}, u32[]{:S(2)}) copy-start(bf16[784,1024]{1,0:T(8,128)(2,1)} %param.31) | copy-start | bytes 4816900
  415.2 41.3 %copy-start.8 = (f32[784,1024]{1,0:T(8,128)S(1)}, f32[784,1024]{1,0:T(8,128)}, u32[]{:S(2)}) copy-start(f32[784,1024]{1,0:T(8,128)} %copy-done.7) | copy-start | bytes 9633796
  415.2 41.3 %copy-start.38 = (bf16[1024,4096]{1,0:T(8,128)(2,1)S(1)}, bf16[1024,4096]{1,0:T(8,128)(2,1)}, u32[]{:S(2)}) copy-start(bf16[1024,4096]{1,0:T(8,128)(2,1)} %all-gather.18.cloned.1.call-done) | copy-start | bytes 25165828
  475.1 298.0 %reduce-scatter.5.cloned.1.call-start = ((), (), s32[]{:S(2)}) async-start(), calls=%async_computation.8 | async-start | bytes 14155776 | tf_op jit(solution)/shard_map/reduce_scatter | solution.py:219
  563.4 495.8 %reduce-scatter.9.cloned.1.call-start = ((), (), s32[]{:S(2)}) async-start(), calls=%async_computation.10 | async-start | bytes 18874368 | tf_op jit(solution)/shard_map/reduce_scatter | solution.py:157
  579.9 764.9 %reduce-scatter.11.cloned.1.call-start = ((), (), s32[]{:S(2)}) async-start(), calls=%async_computation.11 | async-start | bytes 18874368 | tf_op jit(solution)/shard_map/reduce_scatter | solution.py:159
  604.1 812.6 %all-reduce.14.cloned.1.call-start = ((), (), s32[]{:S(2)}) async-start(), calls=%async_computation.12 | async-start | bytes 6291456 | tf_op jit(solution)/shard_map/psum | solution.py:228
  775.5 572.0 %copy-start.9 = (f32[784,1024]{1,0:T(8,128)S(1)}, f32[784,1024]{1,0:T(8,128)}, u32[]{:S(2)}) copy-start(f32[784,1024]{1,0:T(8,128)} %copy-done.7) | copy-start | bytes 9633796
  (38 other events, 282.2 us)
Sparse Core Ops, SparseCore 0:
  10.8 101.9 all-gather.13
  115.5 47.7 all-gather.15
  166.0 123.4 all-gather.17
  292.0 123.1 all-gather.19
  475.2 86.0 reduce-scatter.6
  565.2 207.8 reduce-scatter.4
  777.4 281.7 reduce-scatter.8
  1063.0 281.7 reduce-scatter.10
  1348.7 68.0 all-reduce.13
where the time goes:
time: 1440 us; the launch traced here: 1430 us
  waiting for transfers between devices  858 us (60%)
  blocking collectives  214 us (15%)
  matrix products  187 us (13%)
  local copies, waits for them, and re-layouts  84.6 us (6%)
  other arithmetic  71.7 us (5%)
  between operations  16.1 us (1%)
    reduce_scatter x1, waiting for transfers between devices, local(): lax.psum_scatter(grad_w_fc1, 'fsdp', scatter_dimension=0, tiled=True)  284 us
    reduce_scatter x1, waiting for transfers between devices, local(): lax.psum_scatter(grad_w_fc2, 'fsdp', scatter_dimension=0, tiled=True)  283 us
    all_gather x1, waiting for transfers between devices, local(): lax.all_gather(w_fc2.astype(half), 'fsdp', axis=0, tiled=True)  112 us
    reduce_scatter x1, waiting for transfers between devices, local(): lax.psum_scatter(grad_w_qkv, 'fsdp', scatter_dimension=0, tiled=True)  80.1 us
    dot_general x4, matrix products, times_transposed(): lax.dot_general(left, right, (((1,), (1,)), ((), ())), preferred_element_...  66.1 us
    psum x1, waiting for transfers between devices, local(): lax.psum(attn_shards[0].astype(jnp.bfloat16), 'dp').astype(jnp.float32)  57.2 us
    dot_general x4, matrix products, inner_rows(): lax.dot_general(left, right, (((0,), (0,)), ((), ())), preferred_element_...  44.7 us
    all_gather x1, waiting for transfers between devices, local(): lax.all_gather(w_fc1.astype(half), 'fsdp', axis=0, tiled=True)  41.3 us
  transfers between devices with their start and end apart: 9, of which 6 were waited for; matrix products, arithmetic and copies ran while one was open for 18% of the time, Pallas kernels for 0%

commit v1 on v0

--- a/solution.py
+++ b/solution.py
@@ -225,7 +225,9 @@
         lax.psum_scatter(grad_shift_one, "fsdp", scatter_dimension=0, tiled=True),
     )
     summed = (
-        lax.psum(attn_shards[0].astype(jnp.bfloat16), "dp").astype(jnp.float32),
+        jnp.sum(lax.all_gather(attn_shards[0].astype(jnp.bfloat16), "dp"), axis=0).astype(
+            jnp.float32
+        ),
         lax.psum(attn_shards[1].astype(jnp.bfloat16), "dp").astype(jnp.float32),
         lax.psum(attn_shards[2].astype(jnp.bfloat16), "dp").astype(jnp.float32),
         lax.psum(attn_shards[3].astype(jnp.bfloat16), "dp").astype(jnp.float32),

time: 1440 us -> 1530 us (1.062)
  waiting for transfers between devices: 858 us -> 956 us
    reduce_scatter x1, waiting for transfers between devices: 80.1 us -> 158 us  [local(): lax.psum_scatter(grad_w_qkv, 'fsdp', scatter_dimension=0, tiled=True)]
  transfers between devices with their start and end apart: 9 -> 10, of which waited for: 6 -> 8; matrix products, arithmetic and copies ran while one was open for 18% -> 12% of each run, Pallas kernels for 0% -> 0%
where the time goes in v1:
time: 1530 us
  waiting for transfers between devices  956 us (62%)
  blocking collectives  212 us (14%)
  matrix products  187 us (12%)
  local copies, waits for them, and re-layouts  84 us (5%)
  other arithmetic  70.9 us (5%)
  between operations  16.5 us (1%)
    reduce_scatter x1, waiting for transfers between devices, local(): lax.psum_scatter(grad_w_fc1, 'fsdp', scatter_dimension=0, tiled=True)  285 us
    reduce_scatter x1, waiting for transfers between devices, local(): lax.psum_scatter(grad_w_fc2, 'fsdp', scatter_dimension=0, tiled=True)  283 us
    reduce_scatter x1, waiting for transfers between devices, local(): lax.psum_scatter(grad_w_qkv, 'fsdp', scatter_dimension=0, tiled=True)  158 us
    all_gather x1, waiting for transfers between devices, local(): lax.all_gather(w_fc2.astype(half), 'fsdp', axis=0, tiled=True)  112 us
    dot_general x4, matrix products, times_transposed(): lax.dot_general(left, right, (((1,), (1,)), ((), ())), preferred_element_...  64.2 us
    psum x1, waiting for transfers between devices, local(): lax.psum(attn_shards[3].astype(jnp.bfloat16), 'dp').astype(jnp.float32)  55.9 us
    dot_general x4, matrix products, inner_rows(): lax.dot_general(left, right, (((0,), (0,)), ((), ())), preferred_element_...  47.5 us
    all_gather x1, waiting for transfers between devices, local(): lax.all_gather(w_fc1.astype(half), 'fsdp', axis=0, tiled=True)  40.6 us
  transfers between devices with their start and end apart: 10, of which 8 were waited for; matrix products, arithmetic and copies ran while one was open for 12% of the time, Pallas kernels for 0%

profile of v1, /device:TPU:0, one launch (start us, length us, event | category | flops | bytes accessed | tf_op | source)
XLA Modules:
  0.0 1526.6 jit_solution(17872143167774714685)
XLA Ops:
  16.1 22.5 %all-gather.7 = bf16[8,1,128]{2,1,0:T(2,128)(2,1)S(1)} all-gather(bf16[1,1,128]{2,1,0:T(2,128)(2,1)S(1)} %convert_bitcast_fusion.3), channel_id=1, replica_groups=mesh['dp'=4,'fsdp'=8] {'fsdp'}, dimensions={0}, use_global_device_ids=true | all-gather | bytes 2304 | tf_op jit(solution)/shard_map/all_gather | solution.py:122
  38.6 16.3 %all-gather.6 = bf16[8,1,128]{2,1,0:T(2,128)(2,1)S(1)} all-gather(bf16[1,1,128]{2,1,0:T(2,128)(2,1)S(1)} %convert_bitcast_fusion.4), channel_id=1, replica_groups=mesh['dp'=4,'fsdp'=8] {'fsdp'}, dimensions={0}, use_global_device_ids=true | all-gather | bytes 2304 | tf_op jit(solution)/shard_map/all_gather | solution.py:121
  54.9 18.5 %all-gather.2 = bf16[8,1,128]{2,1,0:T(2,128)(2,1)S(1)} all-gather(bf16[1,1,128]{2,1,0:T(2,128)(2,1)S(1)} %convert_bitcast_fusion.8), channel_id=1, replica_groups=mesh['dp'=4,'fsdp'=8] {'fsdp'}, dimensions={0}, use_global_device_ids=true | all-gather | bytes 2304 | tf_op jit(solution)/shard_map/all_gather | solution.py:87
  73.4 16.4 %all-gather.1 = bf16[8,1,128]{2,1,0:T(2,128)(2,1)S(1)} all-gather(bf16[1,1,128]{2,1,0:T(2,128)(2,1)S(1)} %convert_bitcast_fusion.9), channel_id=1, replica_groups=mesh['dp'=4,'fsdp'=8] {'fsdp'}, dimensions={0}, use_global_device_ids=true | all-gather | bytes 2304 | tf_op jit(solution)/shard_map/all_gather | solution.py:86
  89.9 18.4 %all-gather.5 = bf16[8,1,128]{2,1,0:T(2,128)(2,1)S(1)} all-gather(bf16[1,1,128]{2,1,0:T(2,128)(2,1)S(1)} %convert_bitcast_fusion.5), channel_id=1, replica_groups=mesh['dp'=4,'fsdp'=8] {'fsdp'}, dimensions={0}, use_global_device_ids=true | all-gather | bytes 2304 | tf_op jit(solution)/shard_map/all_gather | solution.py:85
  108.3 16.2 %all-gather.4 = bf16[8,1,128]{2,1,0:T(2,128)(2,1)S(1)} all-gather(bf16[1,1,128]{2,1,0:T(2,128)(2,1)S(1)} %convert_bitcast_fusion.6), channel_id=1, replica_groups=mesh['dp'=4,'fsdp'=8] {'fsdp'}, dimensions={0}, use_global_device_ids=true | all-gather | bytes 2304 | tf_op jit(solution)/shard_map/all_gather | solution.py:83
  124.5 18.2 %all-gather.3 = bf16[8,1,128]{2,1,0:T(2,128)(2,1)S(1)} all-gather(bf16[1,1,128]{2,1,0:T(2,128)(2,1)S(1)} %convert_bitcast_fusion.7), channel_id=1, replica_groups=mesh['dp'=4,'fsdp'=8] {'fsdp'}, dimensions={0}, use_global_device_ids=true | all-gather | bytes 2304 | tf_op jit(solution)/shard_map/all_gather | solution.py:82
  142.8 26.3 %all-gather.8 = bf16[8,1,512]{2,1,0:T(2,128)(2,1)S(1)} all-gather(bf16[1,1,512]{2,1,0:T(2,128)(2,1)S(1)} %reshape.248), channel_id=1, replica_groups=mesh['dp'=4,'fsdp'=8] {'fsdp'}, dimensions={0}, use_global_device_ids=true | all-gather | bytes 9216 | tf_op jit(solution)/shard_map/all_gather | solution.py:118
  187.9 12.8 reshape.268
  248.8 40.6 %all-gather.20.cloned.1.call-done = bf16[1024,4096]{1,0:T(8,128)(2,1)} async-done(((bf16[128,4096]{1,0:T(8,128)(2,1)}), bf16[1024,4096]{1,0:T(8,128)(2,1)}) %all-gather.20.cloned.1.call-update) | async-done | bytes 8388624 | tf_op jit(solution)/shard_map/all_gather | solution.py:117
  289.4 13.3 fusion.42
  302.7 112.4 %all-gather.22.cloned.1.call-done = bf16[4096,1024]{1,0:T(8,128)(2,1)} async-done(((bf16[512,1024]{1,0:T(8,128)(2,1)}), bf16[4096,1024]{1,0:T(8,128)(2,1)}) %all-gather.22.cloned.1.call-update) | async-done | bytes 8388624 | tf_op jit(solution)/shard_map/all_gather | solution.py:119
  415.1 41.2 %convert_reduce_fusion = (f32[4096]{0:T(1024)}, bf16[784,4096]{1,0:T(8,128)(2,1)}, f32[784,4096]{1,0:T(8,128)}) fusion(f32[784,4096]{1,0:T(8,128)} %fusion.42, f32[4096]{0:T(1024)S(1)} %bitcast.99, bf16[784,1024]{1,0:T(8,128)(2,1)S(1)} %copy-done.15, bf16[4096,1024]{1,0:T(8,128)(2,1)} %all-gather.22.cloned.1.call-done), kind=kOutput, calls=%fused_computation.7 | convolution fusion | flops 6817509376 | bytes 42139648 | tf_op jit(solution)/shard_map/dot_general | solution.py:45
  490.9 14.2 multiply_reduce_fusion
  527.7 12.6 convert_element_type.287
  540.4 13.4 fusion.40
  561.3 15.8 %fusion.41 = f32[1024,4096]{1,0:T(8,128)} fusion(bf16[784,4096]{1,0:T(8,128)(2,1)} %get-tuple-element.45, f32[784,1024]{1,0:T(8,128)} %copy-done.9, f32[1024]{0:T(1024)S(1)} %bitcast.112, f32[1024]{0:T(1024)S(1)} %bitcast.108, f32[784]{0:T(1024)S(1)} %fusion.33, f32[784]{0:T(1024)S(1)} %broadcast_multiply_fusion), kind=kOutput, calls=%fused_computation.116 | convolution fusion | flops 6580682752 | bytes 26425472 | tf_op jit(solution)/shard_map/dot_general | solution.py:39
  601.5 157.9 %reduce-scatter.5.cloned.1.call-done = f32[128,3072]{1,0:T(8,128)} async-done(((f32[1024,3072]{1,0:T(8,128)}), f32[128,3072]{1,0:T(8,128)}) %reduce-scatter.5.cloned.1.call-update) | async-done | bytes 1572880 | tf_op jit(solution)/shard_map/reduce_scatter | solution.py:219
  763.7 18.8 %all-gather.9 = bf16[8,1,128]{2,1,0:T(2,128)(2,1)S(1)} all-gather(bf16[1,1,128]{2,1,0:T(2,128)(2,1)S(1)} %convert_bitcast_fusion.2), channel_id=1, replica_groups=mesh['dp'=4,'fsdp'=8] {'fsdp'}, dimensions={0}, use_global_device_ids=true | all-gather | bytes 2304 | tf_op jit(solution)/shard_map/all_gather | solution.py:120
  799.8 34.0 %all-reduce.9 = (bf16[1024]{0:T(1024)(128)(2,1)S(1)}, bf16[1024]{0:T(1024)(128)(2,1)S(1)}, bf16[1024]{0:T(1024)(128)(2,1)S(1)}, bf16[1024]{0:T(1024)(128)(2,1)S(...) all-reduce(f32[1024]{0:T(1024)S(1)} %get-tuple-element.20, ...), channel_id=4, replica_groups=mesh['dp'=4,'fsdp'=8] {'fsdp'}, use_global_device_ids=true, to_apply=%region_14.15.clone | all-reduce | flops 12288 | bytes 73728
  853.4 284.8 %reduce-scatter.9.cloned.1.call-done = f32[128,4096]{1,0:T(8,128)} async-done(((f32[1024,4096]{1,0:T(8,128)}), f32[128,4096]{1,0:T(8,128)}) %reduce-scatter.9.cloned.1.call-update) | async-done | bytes 2097168 | tf_op jit(solution)/shard_map/reduce_scatter | solution.py:157
  1140.9 282.8 %reduce-scatter.11.cloned.1.call-done = f32[512,1024]{1,0:T(8,128)} async-done(((f32[4096,1024]{1,0:T(8,128)}), f32[512,1024]{1,0:T(8,128)}) %reduce-scatter.11.cloned.1.call-update) | async-done | bytes 2097168 | tf_op jit(solution)/shard_map/reduce_scatter | solution.py:159
  1438.4 15.1 all-gather.24.cloned.1.call-done
  1457.4 55.9 %all-reduce.14.cloned.1.call-done = (bf16[128,1024]{1,0:T(8,128)(2,1)}, bf16[128,4096]{1,0:T(8,128)(2,1)}, bf16[512,1024]{1,0:T(8,128)(2,1)}) async-done(((bf16[128,1024]{1,0:T(8,128)(2,1)}, bf16[128,4096]{1,0:T(8,128)(2,1)}, bf16[512,1024]{1,0:T(8,128)(2,1)}), (bf16[128,1024]{1,0:T(8,128)(2,1)}, bf16[128,4096]{1,0:T(8,128)(2,1)}, bf16[512,1024]{1,0:T(8,128)(2,1)})) %all-reduce.14.cloned.1.call-update) | async-done | bytes 2359312 | tf_op jit(solution)/shard_map/psum | solution.py:233
  (241 shorter events, 231.8 us)
Async XLA Ops:
  7.2 170.1 %all-gather.16.cloned.1.call-start = ((), (), s32[]{:S(2)}) async-start(), calls=%async_computation.4 | async-start | bytes 7077888 | tf_op jit(solution)/shard_map/all_gather | solution.py:81
  9.8 231.3 %all-gather.18.cloned.1.call-start = ((), (), s32[]{:S(2)}) async-start(), calls=%async_computation.5 | async-start | bytes 2359296 | tf_op jit(solution)/shard_map/all_gather | solution.py:84
  11.7 43.2 %copy-start.42 = (f32[128]{0:T(128)S(1)}, f32[128]{0:T(128)}, u32[]{:S(2)}) copy-start(f32[128]{0:T(128)} %param.24) | copy-start | bytes 1540
  11.7 61.7 %copy-start.43 = (f32[128]{0:T(128)S(1)}, f32[128]{0:T(128)}, u32[]{:S(2)}) copy-start(f32[128]{0:T(128)} %param.23) | copy-start | bytes 1540
  11.7 78.1 %copy-start.44 = (f32[128]{0:T(128)S(1)}, f32[128]{0:T(128)}, u32[]{:S(2)}) copy-start(f32[128]{0:T(128)} %param.22) | copy-start | bytes 1540
  11.7 96.5 %copy-start.45 = (f32[128]{0:T(128)S(1)}, f32[128]{0:T(128)}, u32[]{:S(2)}) copy-start(f32[128]{0:T(128)} %param.20) | copy-start | bytes 1540
  11.7 112.7 %copy-start.46 = (f32[128]{0:T(128)S(1)}, f32[128]{0:T(128)}, u32[]{:S(2)}) copy-start(f32[128]{0:T(128)} %param.19) | copy-start | bytes 1540
  11.7 130.9 %copy-start.47 = (s32[4]{0:T(128)S(1)}, s32[4]{0:T(128)}, u32[]{:S(2)}) copy-start(s32[4]{0:T(128)} %param.17) | copy-start | bytes 52
  11.7 277.6 %all-gather.20.cloned.1.call-start = ((), (), s32[]{:S(2)}) async-start(), calls=%async_computation.6 | async-start | bytes 9437184 | tf_op jit(solution)/shard_map/all_gather | solution.py:117
  12.9 402.2 %all-gather.22.cloned.1.call-start = ((), (), s32[]{:S(2)}) async-start(), calls=%async_computation.7 | async-start | bytes 9437184 | tf_op jit(solution)/shard_map/all_gather | solution.py:119
  15.7 743.6 %reduce-scatter.5.cloned.1.call-start = ((), (), s32[]{:S(2)}) async-start(), calls=%async_computation.8 | async-start | bytes 14155776 | tf_op jit(solution)/shard_map/reduce_scatter | solution.py:219
  38.5 250.8 %copy-start.33 = (f32[8,1,128]{2,1,0:T(1,128)}, f32[8,1,128]{2,1,0:T(1,128)S(1)}, u32[]{:S(2)}) copy-start(f32[8,1,128]{2,1,0:T(1,128)S(1)} %convert_element_type.322) | copy-start | bytes 12292
  73.4 103.9 %copy-start.35 = (f32[8,1,128]{2,1,0:T(1,128)}, f32[8,1,128]{2,1,0:T(1,128)S(1)}, u32[]{:S(2)}) copy-start(f32[8,1,128]{2,1,0:T(1,128)S(1)} %convert_element_type.319) | copy-start | bytes 12292
  89.8 87.5 %copy-start.28 = (f32[8,1,128]{2,1,0:T(1,128)}, f32[8,1,128]{2,1,0:T(1,128)S(1)}, u32[]{:S(2)}) copy-start(f32[8,1,128]{2,1,0:T(1,128)S(1)} %convert_element_type.318) | copy-start | bytes 12292
  289.4 125.7 %copy-start.15 = (bf16[784,1024]{1,0:T(8,128)(2,1)S(1)}, bf16[784,1024]{1,0:T(8,128)(2,1)}, u32[]{:S(2)}) copy-start(bf16[784,1024]{1,0:T(8,128)(2,1)} %param.31) | copy-start | bytes 4816900
  415.1 41.2 %copy-start.38 = (bf16[1024,4096]{1,0:T(8,128)(2,1)S(1)}, bf16[1024,4096]{1,0:T(8,128)(2,1)}, u32[]{:S(2)}) copy-start(bf16[1024,4096]{1,0:T(8,128)(2,1)} %all-gather.20.cloned.1.call-done) | copy-start | bytes 25165828
  553.7 297.9 %reduce-scatter.7.cloned.1.call-start = ((), (), s32[]{:S(2)}) async-start(), calls=%async_computation.9 | async-start | bytes 4718592 | tf_op jit(solution)/shard_map/reduce_scatter | solution.py:222
  560.6 577.6 %reduce-scatter.9.cloned.1.call-start = ((), (), s32[]{:S(2)}) async-start(), calls=%async_computation.10 | async-start | bytes 18874368 | tf_op jit(solution)/shard_map/reduce_scatter | solution.py:157
  577.0 846.7 %reduce-scatter.11.cloned.1.call-start = ((), (), s32[]{:S(2)}) async-start(), calls=%async_computation.11 | async-start | bytes 18874368 | tf_op jit(solution)/shard_map/reduce_scatter | solution.py:159
  601.4 160.4 %copy-start.49 = (u32[32]{0:T(128)S(1)}, u32[32]{0:T(128)}, u32[]{:S(2)}) copy-start(u32[32]{0:T(128)} %constant.116) | copy-start | bytes 388
  601.4 162.3 %copy-start.48 = (f32[128]{0:T(128)S(1)}, f32[128]{0:T(128)}, u32[]{:S(2)}) copy-start(f32[128]{0:T(128)} %param.28) | copy-start | bytes 1540
  601.4 852.1 %all-gather.24.cloned.1.call-start = ((), (), s32[]{:S(2)}) async-start(), calls=%async_computation.12 | async-start | bytes 3932160 | tf_op jit(solution)/shard_map/all_gather | solution.py:228
  761.8 751.6 %all-reduce.14.cloned.1.call-start = ((), (), s32[]{:S(2)}) async-start(), calls=%async_computation.13 | async-start | bytes 4718592 | tf_op jit(solution)/shard_map/psum | solution.py:233
  853.4 573.0 %copy-start.11 = (f32[784,1024]{1,0:T(8,128)S(1)}, f32[784,1024]{1,0:T(8,128)}, u32[]{:S(2)}) copy-start(f32[784,1024]{1,0:T(8,128)} %copy-done.9) | copy-start | bytes 9633796
  (40 other events, 365.9 us)
Sparse Core Ops, SparseCore 0:
  10.8 101.9 all-gather.15
  115.5 47.7 all-gather.17
  166.0 123.3 all-gather.19
  291.9 123.1 all-gather.21
  553.9 205.4 reduce-scatter.4
  762.8 88.7 reduce-scatter.6
  855.9 282.2 reduce-scatter.8
  1142.0 281.6 reduce-scatter.10
  1425.9 27.5 all-gather.23
  1457.2 56.0 all-reduce.13
